TPU v7x, 32 devices: a whole 2x2x4 slice. The times are simulated.
32 devices in a mesh: dp: 8 (over z, x), tensor: 4 (over y, core).
Axes of the slice: x: 2, y: 2, z: 4, core: 2. Of those that a mesh axis runs over, the one named last changes fastest.
Arguments:
- inputs: bfloat16 [2, 2048, 1280], P(None, 'dp'), may hold values from -6 to 6
- cotangent: bfloat16 [2, 2048, 1280], P(None, 'dp'), may hold values from -0.625 to 0.625
- w_in: bfloat16 [1280, 5120], P('dp', 'tensor'), may hold values from -0.15625 to 0.15625
- w_out: bfloat16 [1280, 5120], P('dp', 'tensor'), may hold values from -0.078125 to 0.078125
- grad_in: float32 [1280, 5120], P('dp', 'tensor'), may hold values from -24 to 24
- grad_out: float32 [1280, 5120], P('dp', 'tensor'), may hold values from -24 to 24
Outputs:
- branch_output: bfloat16 [2, 2048, 1280], P(None, 'dp', 'tensor')
- ascent_in: float32 [1280, 5120], P('dp', 'tensor')
- ascent_out: float32 [1280, 5120], P('dp', 'tensor')
- new_grad_in: float32 [1280, 5120], P('dp', 'tensor')
- new_grad_out: float32 [1280, 5120], P('dp', 'tensor')
All inputs are finite; a program needn't handle non-finite values.
Results may differ from a plain program's by a relative error of at most 0.0064.
Values may be sent and summed in bfloat16 or wider, within the bound.
A program may use at most 128 MiB of HBM per device.

v0:
```python
import math
import jax
import jax.numpy as jnp
from jax import lax
from jax.sharding import PartitionSpec as P

D = 1280
FF = 5120
RHO = 0.1
ETA = 0.01


def gelu_parts(pre):
    cdf = 0.5 * (1.0 + lax.erf(pre * 0.7071067811865476))
    dens = jnp.exp(-0.5 * pre * pre) * 0.3989422804014327
    return (pre * cdf, cdf + pre * dens)


def token_product(left, right):
    return lax.dot_general(
        left, right, (((0,), (0,)), ((), ())), preferred_element_type=jnp.float32
    )


def local(inputs, cotangent, w_in, w_out, grad_in, grad_out):
    scale_in = jnp.abs(w_in.astype(jnp.float32)) + ETA
    scale_out = jnp.abs(w_out.astype(jnp.float32)) + ETA
    scaled_in = scale_in * grad_in
    scaled_out = scale_out * grad_out
    partial_sq = jnp.sum(scaled_in * scaled_in) + jnp.sum(scaled_out * scaled_out)
    row_total = lax.psum(partial_sq, "tensor")
    total = lax.psum(row_total, "dp")
    factor = math.sqrt(2.0 * D * FF) / jnp.sqrt(total + 1.0)
    ascent_in = factor * scaled_in
    ascent_out = factor * scaled_out
    moved_in = (w_in.astype(jnp.float32) + RHO * scale_in * ascent_in).astype(jnp.bfloat16)
    moved_out = (w_out.astype(jnp.float32) + RHO * scale_out * ascent_out).astype(jnp.bfloat16)
    micro = inputs.shape[0]
    full_in, full_out = (
        lax.all_gather(moved_in, "dp", axis=0, tiled=True),
        lax.all_gather(moved_out, "dp", axis=0, tiled=True),
    )
    outputs = []
    acts = []
    deltas = []
    for index in range(micro):
        rows = inputs[index]
        grads_y = cotangent[index]
        pre = jnp.dot(rows, full_in, preferred_element_type=jnp.float32)
        act, slope = gelu_parts(pre)
        act = act.astype(jnp.bfloat16)
        partial_y = lax.dot_general(
            act, full_out, (((1,), (1,)), ((), ())), preferred_element_type=jnp.float32
        )
        shared_y = lax.psum_scatter(partial_y, "tensor", scatter_dimension=1, tiled=True)
        outputs.append(shared_y.astype(jnp.bfloat16))
        back = jnp.dot(grads_y, full_out, preferred_element_type=jnp.float32)
        acts.append(act)
        deltas.append((back * slope).astype(jnp.bfloat16))
    branch_output = jnp.stack(outputs)
    flat_x = inputs.reshape(-1, inputs.shape[2])
    flat_dy = cotangent.reshape(-1, cotangent.shape[2])
    flat_delta = jnp.concatenate(deltas, axis=0)
    flat_act = jnp.concatenate(acts, axis=0)
    whole_in = token_product(flat_x, flat_delta)
    whole_out = token_product(flat_dy, flat_act)
    new_in, new_out = (
        lax.psum_scatter(whole_in, "dp", scatter_dimension=0, tiled=True),
        lax.psum_scatter(whole_out, "dp", scatter_dimension=0, tiled=True),
    )
    return (branch_output, ascent_in, ascent_out, new_in, new_out)


def solution(mesh):
    return jax.shard_map(
        local,
        mesh=mesh,
        in_specs=(
            P(None, "dp", None),
            P(None, "dp", None),
            P("dp", "tensor"),
            P("dp", "tensor"),
            P("dp", "tensor"),
            P("dp", "tensor"),
        ),
        out_specs=(
            P(None, "dp", "tensor"),
            P("dp", "tensor"),
            P("dp", "tensor"),
            P("dp", "tensor"),
            P("dp", "tensor"),
        ),
        check_vma=False,
    )
```

profile of v0, /device:TPU:0, one launch (start us, length us, event | category | flops | bytes accessed | tf_op | source)
XLA Modules:
  0.0 481.0 jit_solution(9765077952277714172)
XLA Ops:
  7.2 0.0 copy-start
  7.2 0.0 copy-start.2
  7.2 0.0 all-gather.3.cloned.1.call-start
  7.2 2.6 multiply_reduce_fusion
  11.2 8.9 %psum.14 = f32[]{:T(128)} all-reduce(f32[]{:T(128)S(6)} %add.44), channel_id=1, replica_groups=mesh['dp'=8,'tensor'=4] {'tensor'}, use_global_device_ids=true, to_apply=%region_2.0 | all-reduce | flops 1 | bytes 8 | tf_op jit(solution)/shard_map/psum | solution.py:31
  20.1 22.3 %psum.15 = f32[]{:T(128)} all-reduce(f32[]{:T(128)} %psum.14), channel_id=1, replica_groups=mesh['dp'=8,'tensor'=4] {'dp'}, use_global_device_ids=true, to_apply=%region_3.0 | all-reduce | flops 1 | bytes 8 | tf_op jit(solution)/shard_map/psum | solution.py:32
  43.0 0.0 copy-start.1
  43.1 0.0 copy-start.3
  43.1 1.2 fusion.22
  44.3 0.0 all-gather.3.cloned.1.call-update
  44.3 0.0 all-gather.5.cloned.1.call-start
  44.4 0.2 copy-done.3
  44.6 1.2 fusion.27
  45.8 0.0 all-gather.5.cloned.1.call-update
  45.8 0.0 reduce-scatter.11.cloned.1.call-start
  45.9 56.3 %all-gather.3.cloned.1.call-done = bf16[1280,1280]{1,0:T(8,128)(2,1)} async-done(((bf16[160,1280]{1,0:T(8,128)(2,1)}), bf16[1280,1280]{1,0:T(8,128)(2,1)}) %all-gather.3.cloned.1.call-update) | async-done | bytes 3276816 | tf_op jit(solution)/shard_map/all_gather | solution.py:40
  102.2 4.2 multiply_convert_fusion
  106.4 58.7 %all-gather.5.cloned.1.call-done = bf16[1280,1280]{1,0:T(8,128)(2,1)} async-done(((bf16[160,1280]{1,0:T(8,128)(2,1)}), bf16[1280,1280]{1,0:T(8,128)(2,1)}) %all-gather.5.cloned.1.call-update) | async-done | bytes 3276816 | tf_op jit(solution)/shard_map/all_gather | solution.py:41
  165.1 4.1 fusion.43
  169.2 0.0 copy-done.7
  169.2 0.0 reduce-scatter.11.cloned.1.call-update
  169.2 0.0 reduce-scatter.9.cloned.1.call-start
  169.2 4.4 multiply_convert_fusion.1
  173.6 0.8 copy-done.8
  174.5 2.1 fusion.42
  176.6 0.0 reduce-scatter.9.cloned.1.call-update
  176.6 0.0 reduce-scatter.15.cloned.1.call-start
  176.7 6.4 %convolution_bitcast_fusion = f32[1280,1280]{0,1:T(8,128)} fusion(bf16[512,1280]{1,0:T(8,128)(2,1)} %bitcast.54, bf16[256,1280]{1,0:T(8,128)(2,1)} %copy-done.7, bf16[256,1280]{1,0:T(8,128)(2,1)} %copy-done.8), kind=kOutput, calls=%fused_computation | convolution fusion | flops 1680343040 | bytes 9175040 | tf_op jit(solution)/shard_map/dot_general | solution.py:20
  183.0 8.2 %copy.17 = f32[1280,1280]{1,0:T(8,128)} copy(f32[1280,1280]{0,1:T(8,128)} %convolution_bitcast_fusion) | data formatting | bytes 13107200
  191.3 0.0 reduce-scatter.15.cloned.1.call-update
  191.3 0.0 reduce-scatter.13.cloned.1.call-start
  191.3 0.0 copy-start.5
  191.4 0.0 copy-start.9
  191.4 2.8 fusion.3
  194.2 0.0 copy-done.5
  194.2 0.0 copy-start.6
  194.2 1.1 fusion.2
  195.3 0.2 copy-done.6
  195.5 4.6 convolution_bitcast_fusion.1
  200.1 8.3 %copy.15 = f32[1280,1280]{1,0:T(8,128)} copy(f32[1280,1280]{0,1:T(8,128)} %convolution_bitcast_fusion.1) | data formatting | bytes 13107200
  208.4 0.0 reduce-scatter.13.cloned.1.call-update
  208.4 0.0 reduce-scatter.11.cloned.1.call-done
  208.4 1.0 convert_bitcast_fusion
  209.4 13.9 %reduce-scatter.9.cloned.1.call-done = f32[256,320]{0,1:T(8,128)} async-done(((f32[256,1280]{0,1:T(8,128)}), f32[256,320]{0,1:T(8,128)}) %reduce-scatter.9.cloned.1.call-update) | async-done | bytes 327696 | tf_op jit(solution)/shard_map/reduce_scatter | solution.py:55
  223.3 1.0 convert_bitcast_fusion.1
  224.3 0.8 pad_maximum_fusion
  225.0 124.1 %reduce-scatter.15.cloned.1.call-done = f32[160,1280]{1,0:T(8,128)} async-done(((f32[1280,1280]{1,0:T(8,128)}), f32[160,1280]{1,0:T(8,128)}) %reduce-scatter.15.cloned.1.call-update) | async-done | bytes 819216
  349.1 125.1 %reduce-scatter.13.cloned.1.call-done = f32[160,1280]{1,0:T(8,128)} async-done(((f32[1280,1280]{1,0:T(8,128)}), f32[160,1280]{1,0:T(8,128)}) %reduce-scatter.13.cloned.1.call-update) | async-done | bytes 819216
  (8 shorter events, 0.0 us)
Async XLA Ops:
  7.2 35.9 %copy-start = (f32[160,1280]{1,0:T(8,128)S(1)}, f32[160,1280]{1,0:T(8,128)}, u32[]{:S(2)}) copy-start(f32[160,1280]{1,0:T(8,128)} %param.10) | copy-start | bytes 2457604
  7.2 35.9 %copy-start.2 = (bf16[160,1280]{1,0:T(8,128)(2,1)S(1)}, bf16[160,1280]{1,0:T(8,128)(2,1)}, u32[]{:S(2)}) copy-start(bf16[160,1280]{1,0:T(8,128)(2,1)} %param.8) | copy-start | bytes 1228804
  7.2 95.0 %all-gather.3.cloned.1.call-start = ((), (), s32[]{:S(2)}) async-start(), calls=%async_computation.4 | async-start | bytes 3686400 | tf_op jit(solution)/shard_map/all_gather | solution.py:40
  43.0 1.4 copy-start.1
  43.1 1.5 copy-start.3
  44.3 120.8 %all-gather.5.cloned.1.call-start = ((), (), s32[]{:S(2)}) async-start(), calls=%async_computation.5 | async-start | bytes 3686400 | tf_op jit(solution)/shard_map/all_gather | solution.py:41
  45.8 162.6 %reduce-scatter.11.cloned.1.call-start = ((), (), s32[]{:S(2)}) async-start(), calls=%async_computation.7 | async-start | bytes 1638400 | tf_op jit(solution)/shard_map/reduce_scatter | solution.py:55
  106.4 62.8 %copy-start.7 = (bf16[256,1280]{1,0:T(8,128)(2,1)}, bf16[256,1280]{1,0:T(8,128)(2,1)S(1)}, u32[]{:S(2)}) copy-start(bf16[256,1280]{1,0:T(8,128)(2,1)S(1)} %get-tuple-element.19) | copy-start | bytes 1966084
  169.2 5.3 %copy-start.4 = (bf16[1280,1280]{1,0:T(8,128)(2,1)S(1)}, bf16[1280,1280]{1,0:T(8,128)(2,1)}, u32[]{:S(2)}) copy-start(bf16[1280,1280]{1,0:T(8,128)(2,1)} %all-gather.5.cloned.1.call-done) | copy-start | bytes 9830404
  169.2 54.1 %reduce-scatter.9.cloned.1.call-start = ((), (), s32[]{:S(2)}) async-start(), calls=%async_computation.6 | async-start | bytes 1638400 | tf_op jit(solution)/shard_map/reduce_scatter | solution.py:55
  173.6 0.8 copy-start.8
  176.6 172.5 %reduce-scatter.15.cloned.1.call-start = ((), (), s32[]{:S(2)}) async-start(), calls=%async_computation.9 | async-start | bytes 7372800
  191.3 282.8 %reduce-scatter.13.cloned.1.call-start = ((), (), s32[]{:S(2)}) async-start(), calls=%async_computation.8 | async-start | bytes 7372800
  191.3 2.8 copy-start.5
  191.4 2.8 copy-start.9
  194.2 1.3 copy-start.6
Sparse Core Ops, SparseCore 0:
  44.5 57.6 all-gather.2
  104.9 60.1 all-gather.4
  169.3 25.0 reduce-scatter.10
  196.8 26.3 reduce-scatter.8
  227.3 121.7 reduce-scatter.14
  353.1 120.9 reduce-scatter.12
where the time goes:
time: 482 us; the launch traced here: 481 us
  waiting for transfers between devices  378 us (78%)
  blocking collectives  31.2 us (6%)
  matrix products  29.7 us (6%)
  local copies, waits for them, and re-layouts  17.7 us (4%)
  between operations  16.2 us (3%)
  other arithmetic  7.87 us (2%)
    unnamed x8, waiting for transfers between devices  249 us
    all_gather x1, waiting for transfers between devices, local(): lax.all_gather(moved_out, 'dp', axis=0, tiled=True)  58.7 us
    all_gather x1, waiting for transfers between devices, local(): lax.all_gather(moved_in, 'dp', axis=0, tiled=True)  56.3 us
    psum x1, blocking collectives, local(): total = lax.psum(row_total, 'dp')  22.3 us
    unnamed x22, local copies, waits for them, and re-layouts  17.7 us
    reduce_scatter x2, waiting for transfers between devices, local(): lax.psum_scatter(partial_y, 'tensor', scatter_dimension=1, tiled=True)  13.9 us
    dot_general x2, matrix products, token_product(): lax.dot_general(left, right, (((0,), (0,)), ((), ())), preferred_element_...  11 us
  transfers between devices with their start and end apart: 6, of which 5 were waited for; matrix products, arithmetic and copies ran while one was open for 10% of the time, Pallas kernels for 0%

commit v1 on v0

--- a/solution.py
+++ b/solution.py
@@ -8,6 +8,27 @@
 FF = 5120
 RHO = 0.1
 ETA = 0.01
+
+
+def in_order(tiles, dim):
+    dims = list(tiles.shape[1:])
+    dims[dim] *= tiles.shape[0]
+    return jnp.moveaxis(tiles, 0, dim).reshape(dims)
+
+
+def doubled(x, axis):
+    count, position = (lax.axis_size(axis), lax.axis_index(axis))
+    pieces, bit = (x[None], 1)
+    while bit < count:
+        theirs = lax.ppermute(pieces, axis, [(i, i ^ bit) for i in range(count)])
+        low = position & bit == 0
+        pieces = jnp.concatenate([jnp.where(low, pieces, theirs), jnp.where(low, theirs, pieces)])
+        bit *= 2
+    return pieces
+
+
+def gather_by_bits(x, axis, dim):
+    return in_order(doubled(x, axis), dim)
 
 
 def gelu_parts(pre):
@@ -38,7 +59,7 @@
     micro = inputs.shape[0]
     full_in, full_out = (
         lax.all_gather(moved_in, "dp", axis=0, tiled=True),
-        lax.all_gather(moved_out, "dp", axis=0, tiled=True),
+        gather_by_bits(moved_out, "dp", 0),
     )
     outputs = []
     acts = []

time: 482 us -> 498 us (1.033)
  waiting for transfers between devices: 378 us -> 393 us
    ppermute x0 -> x3, waiting for transfers between devices: none -> 130 us  [doubled(): theirs = lax.ppermute(pieces, axis, [(i, i ^ bit) for i in range(count)])]
    all_gather x1 -> x0, waiting for transfers between devices: 58.7 us -> none  [local(): lax.all_gather(moved_out, 'dp', axis=0, tiled=True)]
    all_gather x1, waiting for transfers between devices: 56.3 us -> 0.02 us  [local(): lax.all_gather(moved_in, 'dp', axis=0, tiled=True)]
    unnamed x22 -> x20, local copies, waits for them, and re-layouts: 17.7 us -> 18.6 us
    unnamed x8 -> x7, waiting for transfers between devices: 249 us -> 249 us
  transfers between devices with their start and end apart: 6 -> 8, of which waited for: 5 -> 6; matrix products, arithmetic and copies ran while one was open for 10% -> 9% of each run, Pallas kernels for 0% -> 0%
where the time goes in v1:
time: 498 us; the launch traced here: 497 us
  waiting for transfers between devices  393 us (79%)
  blocking collectives  31.2 us (6%)
  matrix products  27.6 us (6%)
  local copies, waits for them, and re-layouts  18.6 us (4%)
  between operations  16 us (3%)
  other arithmetic  10.1 us (2%)
    unnamed x7, waiting for transfers between devices  249 us
    ppermute x3, waiting for transfers between devices, doubled(): theirs = lax.ppermute(pieces, axis, [(i, i ^ bit) for i in range(count)])  130 us
    psum x1, blocking collectives, local(): total = lax.psum(row_total, 'dp')  22.3 us
    unnamed x20, local copies, waits for them, and re-layouts  18.6 us
    reduce_scatter x2, waiting for transfers between devices, local(): lax.psum_scatter(partial_y, 'tensor', scatter_dimension=1, tiled=True)  13.7 us
    dot_general x2, matrix products, token_product(): lax.dot_general(left, right, (((0,), (0,)), ((), ())), preferred_element_...  11 us
  transfers between devices with their start and end apart: 8, of which 6 were waited for; matrix products, arithmetic and copies ran while one was open for 9% of the time, Pallas kernels for 0%

profile of v1, /device:TPU:0, one launch (start us, length us, event | category | flops | bytes accessed | tf_op | source)
XLA Modules:
  0.0 497.0 jit_solution(6864161073116264421)
XLA Ops:
  7.2 0.0 all-gather.2.cloned.1.call-start
  7.2 2.6 multiply_reduce_fusion
  11.2 8.9 %psum.14 = f32[]{:T(128)} all-reduce(f32[]{:T(128)S(6)} %add.44), channel_id=1, replica_groups=mesh['dp'=8,'tensor'=4] {'tensor'}, use_global_device_ids=true, to_apply=%region_2.0 | all-reduce | flops 1 | bytes 8 | tf_op jit(solution)/shard_map/psum | solution.py:52
  20.1 22.3 %psum.15 = f32[]{:T(128)} all-reduce(f32[]{:T(128)} %psum.14), channel_id=1, replica_groups=mesh['dp'=8,'tensor'=4] {'dp'}, use_global_device_ids=true, to_apply=%region_3.0 | all-reduce | flops 1 | bytes 8 | tf_op jit(solution)/shard_map/psum | solution.py:53
  43.1 1.2 fusion.22
  44.3 0.0 all-gather.2.cloned.1.call-update
  44.3 0.0 reduce-scatter.11.cloned.1.call-start
  44.4 0.2 copy-done.3
  44.6 1.1 fusion.38
  45.7 12.2 %collective-permute-done = bf16[1,160,1280]{2,1,0:T(8,128)(2,1)S(1)} collective-permute-done((bf16[1,160,1280]{2,1,0:T(8,128)(2,1)S(1)}, bf16[1,160,1280]{2,1,0:T(8,128)(2,1)S(1)}, u32[]{:S(2)}, u32[]{:S(2)}) %collective-permute-start) | collective-permute-done | bytes 409632 | tf_op jit(solution)/shard_map/ppermute | solution.py:23
  57.9 0.1 broadcast_select_fusion.5
  57.9 0.1 pad_maximum_fusion.2
  58.0 0.1 collective-permute-start.1
  58.1 22.8 %collective-permute-done.1 = bf16[2,160,1280]{2,1,0:T(8,128)(2,1)S(1)} collective-permute-done((bf16[2,160,1280]{2,1,0:T(8,128)(2,1)S(1)}, bf16[2,160,1280]{2,1,0:T(8,128)(2,1)S(1)}, u32[]{:S(2)}, u32[]{:S(2)}) %collective-permute-start.1) | collective-permute-done | bytes 819232 | tf_op jit(solution)/shard_map/ppermute | solution.py:23
  80.9 0.1 broadcast_select_fusion.3
  81.0 0.1 pad_maximum_fusion.1
  81.2 0.1 collective-permute-start.2
  81.3 95.1 %collective-permute-done.2 = bf16[4,160,1280]{2,1,0:T(8,128)(2,1)} collective-permute-done((bf16[4,160,1280]{2,1,0:T(8,128)(2,1)S(1)}, bf16[4,160,1280]{2,1,0:T(8,128)(2,1)}, u32[]{:S(2)}, u32[]{:S(2)}) %collective-permute-start.2) | collective-permute-done | bytes 1638432 | tf_op jit(solution)/shard_map/ppermute | solution.py:23
  176.4 1.6 broadcast_select_fusion.1
  178.0 0.3 pad_maximum_fusion
  178.3 0.0 all-gather.2.cloned.1.call-done
  178.3 4.2 multiply_convert_fusion
  182.6 0.8 copy-done.6
  183.4 2.1 fusion.44
  185.5 0.0 reduce-scatter.11.cloned.1.call-update
  185.6 0.0 reduce-scatter.9.cloned.1.call-start
  185.6 4.2 multiply_convert_fusion.1
  189.8 0.8 copy-done.7
  190.7 2.1 fusion.43
  192.8 0.0 reduce-scatter.9.cloned.1.call-update
  192.8 0.0 reduce-scatter.15.cloned.1.call-start
  192.9 6.4 %convolution_bitcast_fusion = f32[1280,1280]{0,1:T(8,128)} fusion(bf16[512,1280]{1,0:T(8,128)(2,1)} %bitcast.61, bf16[256,1280]{1,0:T(8,128)(2,1)} %copy-done.6, bf16[256,1280]{1,0:T(8,128)(2,1)} %copy-done.7), kind=kOutput, calls=%fused_computation | convolution fusion | flops 1680343040 | bytes 9175040 | tf_op jit(solution)/shard_map/dot_general | solution.py:41
  199.2 8.3 %copy.17 = f32[1280,1280]{1,0:T(8,128)} copy(f32[1280,1280]{0,1:T(8,128)} %convolution_bitcast_fusion) | data formatting | bytes 13107200
  207.5 0.0 reduce-scatter.15.cloned.1.call-update
  207.5 0.2 reduce-scatter.13.cloned.1.call-start
  207.8 2.8 fusion.3
  210.6 1.1 fusion.2
  211.8 0.2 copy-done.5
  211.9 4.6 convolution_bitcast_fusion.1
  216.5 8.3 %copy.15 = f32[1280,1280]{1,0:T(8,128)} copy(f32[1280,1280]{0,1:T(8,128)} %convolution_bitcast_fusion.1) | data formatting | bytes 13107200
  224.8 0.0 reduce-scatter.13.cloned.1.call-update
  224.8 0.0 reduce-scatter.11.cloned.1.call-done
  224.9 1.0 convert_bitcast_fusion
  225.9 13.6 %reduce-scatter.9.cloned.1.call-done = f32[256,320]{0,1:T(8,128)} async-done(((f32[256,1280]{0,1:T(8,128)}), f32[256,320]{0,1:T(8,128)}) %reduce-scatter.9.cloned.1.call-update) | async-done | bytes 327696 | tf_op jit(solution)/shard_map/reduce_scatter | solution.py:76
  239.5 1.0 convert_bitcast_fusion.1
  240.5 0.8 pad_maximum_fusion.3
  241.3 124.1 %reduce-scatter.15.cloned.1.call-done = f32[160,1280]{1,0:T(8,128)} async-done(((f32[1280,1280]{1,0:T(8,128)}), f32[160,1280]{1,0:T(8,128)}) %reduce-scatter.15.cloned.1.call-update) | async-done | bytes 819216
  365.4 125.1 %reduce-scatter.13.cloned.1.call-done = f32[160,1280]{1,0:T(8,128)} async-done(((f32[1280,1280]{1,0:T(8,128)}), f32[160,1280]{1,0:T(8,128)}) %reduce-scatter.13.cloned.1.call-update) | async-done | bytes 819216
  (15 shorter events, 0.0 us)
Async XLA Ops:
  7.2 35.9 %copy-start = (f32[160,1280]{1,0:T(8,128)S(1)}, f32[160,1280]{1,0:T(8,128)}, u32[]{:S(2)}) copy-start(f32[160,1280]{1,0:T(8,128)} %param.10) | copy-start | bytes 2457604
  7.2 35.9 %copy-start.2 = (bf16[160,1280]{1,0:T(8,128)(2,1)S(1)}, bf16[160,1280]{1,0:T(8,128)(2,1)}, u32[]{:S(2)}) copy-start(bf16[160,1280]{1,0:T(8,128)(2,1)} %param.8) | copy-start | bytes 1228804
  7.2 171.1 %all-gather.2.cloned.1.call-start = ((), (), s32[]{:S(2)}) async-start(), calls=%async_computation.4 | async-start | bytes 3686400 | tf_op jit(solution)/shard_map/all_gather | solution.py:61
  43.0 1.4 copy-start.1
  43.1 1.5 copy-start.3
  44.3 180.5 %reduce-scatter.11.cloned.1.call-start = ((), (), s32[]{:S(2)}) async-start(), calls=%async_computation.6 | async-start | bytes 1638400 | tf_op jit(solution)/shard_map/reduce_scatter | solution.py:76
  45.7 12.2 %collective-permute-start = (bf16[1,160,1280]{2,1,0:T(8,128)(2,1)S(1)}, bf16[1,160,1280]{2,1,0:T(8,128)(2,1)S(1)}, u32[]{:S(2)}, u32[]{:S(2)}) collective-permute-start(bf16[1,160,1280]{2,1,0:T(8,128)(2,1)S(1)} %get-tuple-element.15), channel_id=1, source_target_pairs={{0,4},{4,0},{8,12},{12,8},{16,20},{20,16},{24,28},{28,24},{1,5},{5... | collective-permute-start | bytes 1228808 | tf_op jit(solution)/shard_map/ppermute | solution.py:23
  58.0 22.9 %collective-permute-start.1 = (bf16[2,160,1280]{2,1,0:T(8,128)(2,1)S(1)}, bf16[2,160,1280]{2,1,0:T(8,128)(2,1)S(1)}, u32[]{:S(2)}, u32[]{:S(2)}) collective-permute-start(bf16[2,160,1280]{2,1,0:T(8,128)(2,1)S(1)} %pad_maximum_fusion.2), channel_id=1, source_target_pairs={{0,8},{4,12},{8,0},{12,4},{16,24},{20,28},{24,16},{28,20},{1,9},{5... | collective-permute-start | bytes 2457608 | tf_op jit(solution)/shard_map/ppermute | solution.py:23
  81.2 95.2 %collective-permute-start.2 = (bf16[4,160,1280]{2,1,0:T(8,128)(2,1)S(1)}, bf16[4,160,1280]{2,1,0:T(8,128)(2,1)}, u32[]{:S(2)}, u32[]{:S(2)}) collective-permute-start(bf16[4,160,1280]{2,1,0:T(8,128)(2,1)S(1)} %pad_maximum_fusion.1), channel_id=1, source_target_pairs={{0,16},{4,20},{8,24},{12,28},{16,0},{20,4},{24,8},{28,12},{1,17},{... | collective-permute-start | bytes 4915208 | tf_op jit(solution)/shard_map/ppermute | solution.py:23
  182.6 0.8 copy-start.6
  185.6 54.0 %reduce-scatter.9.cloned.1.call-start = ((), (), s32[]{:S(2)}) async-start(), calls=%async_computation.5 | async-start | bytes 1638400 | tf_op jit(solution)/shard_map/reduce_scatter | solution.py:76
  189.8 0.8 copy-start.7
  192.8 172.6 %reduce-scatter.15.cloned.1.call-start = ((), (), s32[]{:S(2)}) async-start(), calls=%async_computation.8 | async-start | bytes 7372800
  207.5 282.9 %reduce-scatter.13.cloned.1.call-start = ((), (), s32[]{:S(2)}) async-start(), calls=%async_computation.7 | async-start | bytes 7372800
  207.8 2.8 copy-start.4
  207.8 2.8 copy-start.8
  210.6 1.3 copy-start.5
Sparse Core Ops, SparseCore 0:
  44.5 110.3 all-gather.1
  185.7 24.7 reduce-scatter.10
  213.0 26.4 reduce-scatter.8
  243.6 121.7 reduce-scatter.14
  369.4 120.9 reduce-scatter.12
